TPU v7x, 512 devices: a 8x2x16 block of a 8x8x16 slice. The times are simulated.
512 devices in a mesh: groups: 2 (over y), expert: 32 (over z, core), mp: 8 (over x).
Axes of the slice: x: 8, y: 2, z: 16, core: 2. Of those that a mesh axis runs over, the one named last changes fastest.
The devices are a block of a 8x8x16 slice.
Arguments:
- tokens_in: bfloat16 [16384, 2048], P(('groups', 'expert'), 'mp'), parts along dimension 0, may hold values from -6 to 6
- out_grad: bfloat16 [16384, 2048], P(('groups', 'expert'), 'mp'), parts along dimension 0, may hold values from -3 to 3
- logits: float32 [16384, 32], P(('groups', 'expert')), parts along dimension 0, may hold values from -6 to 6
- indices: int32 [64, 256], P('groups'), parts along dimension 0, may hold values from 0 to 8191, as said below
- w_in: bfloat16 [32, 2048, 4096], P('expert', None, 'mp'), may hold values from -0.125 to 0.125
- w_out: bfloat16 [32, 4096, 2048], P('expert', 'mp'), may hold values from -0.09375 to 0.09375
- router_w: bfloat16 [2048, 32], P('mp'), may hold values from -0.125 to 0.125
Outputs:
- input_grad: float32 [16384, 2048], P(('groups', 'expert'), 'mp'), parts along dimension 0
- router_grad: float32 [4096, 32], P(('groups', 'mp')), parts along dimension 0
There are 2 independent parts, one for each index of `groups`. A program takes and returns all parts, laid end to end along the dimension named above; an argument that names none is the same for every part. Nothing has to cross between parts.
Inputs may be any that keep to these rules, and one draw needn't show every extreme that they name: `indices`: each expert's row holds 256 different tokens. Of the 256 tokens of one index of the expert axis (rows k * 256 to (k + 1) * 256 - 1), one expert takes at most 16, and every expert takes exactly 16 from some such index.
All inputs are finite; a program needn't handle non-finite values.
Results may differ from a plain program's by a relative error of at most 0.019.
Values may be sent and summed in bfloat16 or wider, within the bound.
No kernel may reach another device: no remote copies, remote signals or barrier semaphores. Data moves between devices by JAX's collectives and lax.ppermute only.
A program may use at most 64 MiB of HBM per device.

v0:
```python
import jax
import jax.numpy as jnp
from jax import lax
from jax.sharding import PartitionSpec as P

inv_root_two = 0.7071067811865476
inv_root_tau = 0.3989422804014327


def in_one_piece(arrays, axis, split_dim, concat_dim, along):
    widths = [a.shape[along] for a in arrays]
    both = jnp.concatenate(arrays, axis=along)
    result = lax.all_to_all(both, axis, split_axis=split_dim, concat_axis=concat_dim, tiled=True)
    return tuple(jnp.split(result, [sum(widths[:k]) for k in range(1, len(widths))], axis=along))


def joined_along(blocks, dim):
    shape = list(blocks.shape[1:])
    shape[dim] *= blocks.shape[0]
    return jnp.moveaxis(blocks, 0, dim).reshape(shape)


def copy_for_each(x, axis):
    copies = jnp.broadcast_to(x, (lax.axis_size(axis), *x.shape))
    return lax.all_to_all(copies, axis, split_axis=0, concat_axis=0, tiled=True)


def gather_directly(x, axis, dim):
    return joined_along(copy_for_each(x, axis), dim)


def side_by_side(arrays, axis, dim, along):
    both = jnp.concatenate(arrays, axis=along)
    result, at, finished = (gather_directly(both, axis, dim), 0, [])
    for a in arrays:
        finished.append(lax.slice_in_dim(result, at, at + a.shape[along], axis=along))
        at += a.shape[along]
    return tuple(finished)


def in_blocks(x, dim, length):
    shape = x.shape
    blocks = x.reshape(*shape[:dim], length, shape[dim] // length, *shape[dim + 1 :])
    return jnp.moveaxis(blocks, dim, 0)


def summed_on_arrival(x, axis, dim):
    length = lax.axis_size(axis)
    blocks = lax.all_to_all(in_blocks(x, dim, length), axis, 0, 0, tiled=True)
    return jnp.sum(blocks.astype(jnp.float32), axis=0)


def of_everyone(x, axis):
    everything = copy_for_each(x, axis)
    return jnp.sum(everything, axis=0)


def taken_together(x, axis):
    return copy_for_each(x, axis).astype(jnp.float32).sum(axis=0)


def gelu_parts(hidden_pre):
    cumulative = 0.5 * (1.0 + lax.erf(hidden_pre * inv_root_two))
    slopes = cumulative + hidden_pre * jnp.exp(-0.5 * hidden_pre * hidden_pre) * inv_root_tau
    return (hidden_pre * cumulative, slopes)


def per_device(tokens_in, out_grad, logits, indices, w_in, w_out, router_w):
    tok_dev, columns = tokens_in.shape
    experts, capacity = indices.shape
    most_rows = min(tok_dev, 2 * capacity // experts)
    expert_here = lax.axis_index("expert")
    expert_range = jnp.arange(experts, dtype=jnp.int32)
    source = indices // tok_dev
    onehot_src = (source[:, :, None] == expert_range[None, None, :]).astype(jnp.int32)
    earlier = jnp.cumsum(onehot_src, axis=1) - onehot_src
    slot_rank = jnp.sum(earlier * onehot_src, axis=2)
    mine = source == expert_here
    slot_pos = jnp.where(mine, slot_rank, most_rows)
    local_tok = indices - expert_here * tok_dev
    pack_tok = jnp.full((experts, most_rows), -1, jnp.int32)
    pack_tok = pack_tok.at[expert_range[:, None], slot_pos].set(local_tok, mode="drop")
    flat_ok = (pack_tok >= 0).reshape(-1)
    flat_tok = jnp.clip(pack_tok, 0, tok_dev - 1).reshape(-1)
    own_src = lax.dynamic_index_in_dim(source, expert_here, 0, keepdims=False)
    own_rank = lax.dynamic_index_in_dim(slot_rank, expert_here, 0, keepdims=False)
    zero_bf = jnp.zeros((), jnp.bfloat16)
    send_x = jnp.where(flat_ok[:, None], tokens_in[flat_tok], zero_bf)
    send_dy = jnp.where(flat_ok[:, None], out_grad[flat_tok], zero_bf)
    recv_x, recv_dy = in_one_piece((send_x, send_dy), "expert", 0, 0, 1)
    slot_rows = own_src * most_rows + own_rank
    chosen_x = recv_x[slot_rows]
    chosen_dy = recv_dy[slot_rows]
    weight_in = w_in[0]
    weight_out = w_out[0]
    pieces = side_by_side((chosen_x, chosen_dy), "mp", 1, 0)
    rows_in = weight_in
    new_pre = jnp.dot(pieces[0], rows_in, preferred_element_type=jnp.float32)
    new_back = lax.dot_general(
        pieces[1], weight_out, (((1,), (1,)), ((), ())), preferred_element_type=jnp.float32
    )
    activated, slopes = gelu_parts(new_pre)
    gate_part = jnp.sum(activated * new_back, axis=1)
    delta = (new_back * slopes).astype(jnp.bfloat16)
    rows_in = weight_in
    contrib = summed_on_arrival(
        lax.dot_general(
            rows_in, delta, (((1,), (1,)), ((), ())), preferred_element_type=jnp.float32
        ).astype(jnp.bfloat16),
        "mp",
        0,
    ).astype(jnp.bfloat16)
    gate_vals = of_everyone(gate_part, "mp")
    slot_table = (
        jnp.zeros((experts, most_rows), jnp.int32)
        .at[own_src, own_rank]
        .set(jnp.arange(capacity, dtype=jnp.int32))
    )
    filled = jnp.zeros((experts, most_rows), jnp.bool_).at[own_src, own_rank].set(True)
    slot_flat = slot_table.reshape(-1)
    filled_flat = filled.reshape(-1)
    send_contrib = jnp.where(filled_flat[None, :], jnp.take(contrib, slot_flat, axis=1), zero_bf)
    send_gates = jnp.where(filled_flat, gate_vals[slot_flat], 0.0)[None, :]
    recv_contrib, recv_gates = (
        lax.all_to_all(send_contrib, "expert", split_axis=1, concat_axis=1, tiled=True),
        lax.all_to_all(
            send_gates.astype(jnp.bfloat16), "expert", split_axis=1, concat_axis=1, tiled=True
        ).astype(send_gates.dtype),
    )
    gate_probs = jax.nn.sigmoid(logits)
    expert_of = jnp.repeat(expert_range, most_rows)
    gate_slot = jnp.where(flat_ok, gate_probs[flat_tok, expert_of], 0.0)
    scaled_cols = recv_contrib.astype(jnp.float32) * gate_slot[None, :]
    expert_dx = jnp.zeros((columns, tok_dev), jnp.float32).at[:, flat_tok].add(scaled_cols).T
    slot_gates = jnp.where(flat_ok, recv_gates.reshape(-1), 0.0)
    gate_grad = jnp.zeros((tok_dev, experts), jnp.float32).at[flat_tok, expert_of].add(slot_gates)
    logit_grad = (gate_probs * (1.0 - gate_probs) * gate_grad).astype(jnp.bfloat16)
    router_dx = lax.dot_general(
        logit_grad, router_w, (((1,), (1,)), ((), ())), preferred_element_type=jnp.float32
    )
    input_grad = expert_dx + router_dx
    local_router = lax.dot_general(
        tokens_in, logit_grad, (((0,), (0,)), ((), ())), preferred_element_type=jnp.float32
    )
    router_grad = taken_together(local_router.astype(jnp.bfloat16), "expert").astype(jnp.float32)
    return (input_grad, router_grad)


def solution(mesh):
    return jax.shard_map(
        per_device,
        mesh=mesh,
        in_specs=(
            P(("groups", "expert"), "mp"),
            P(("groups", "expert"), "mp"),
            P(("groups", "expert"), None),
            P("groups", None),
            P("expert", None, "mp"),
            P("expert", "mp", None),
            P("mp", None),
        ),
        out_specs=(P(("groups", "expert"), "mp"), P(("groups", "mp"), None)),
        check_vma=False,
    )
```

profile of v0, /device:TPU:65, one launch (start us, length us, event | category | flops | bytes accessed | tf_op | source)
XLA Modules:
  0.0 364.2 jit_solution(2544707056546900622)
XLA Ops:
  0.6 0.9 add_select_fusion
  1.6 1.1 fusion.9
  2.8 32.3 %reduce-window.6 = s32[32,32,2,128]{3,1,2,0:T(8,128)S(1)} reduce-window(s32[32,32,2,128]{3,1,2,0:T(8,128)} %fusion.9, s32[]{:T(128)} %constant.26.clone.1), window={size=1x1x1x128 pad=0_0x0_0x0_0x127_0}, to_apply=%region_0.1 | reduce-window | flops 33292288 | bytes 2097156 | tf_op jit(solution)/shard_map/reduce-window
  35.1 1.3 slice.44
  36.4 1.7 copy.63
  38.2 0.4 fusion.8
  39.0 30.4 %scatter_custom_fusion.4 = s32[512]{0:T(512)S(1)} fusion(s32[8192]{0:T(1024)S(1)} %bitcast.103, s32[8192]{0:T(1024)S(1)} %bitcast.104, s32[]{:T(128)} %constant.27.clone.1), kind=kCustom, calls=%fused_computation.98 | custom fusion | bytes 2052
  69.8 2.0 gather_fusion.1
  71.8 2.0 gather_fusion
  73.9 0.1 broadcast_select_fusion.1
  74.1 0.9 pad_maximum_fusion
  74.9 45.2 %all-to-all-start = ((bf16[32,16,512]{2,1,0:T(8,128)(2,1)}), bf16[32,16,512]{2,1,0:T(8,128)(2,1)S(1)}, u32[]{:S(2)}, u32[]{:S(2)}) async-start(bf16[32,16,512]{2,1,0:T(8,128)(2,1)} %pad_maximum_fusion), calls=%async_computation | async-start | bytes 1048576 | tf_op jit(solution)/shard_map/all_to_all | solution.py:13
  120.2 33.4 %all-to-all-done = bf16[32,16,512]{2,1,0:T(8,128)(2,1)S(1)} async-done(((bf16[32,16,512]{2,1,0:T(8,128)(2,1)}), bf16[32,16,512]{2,1,0:T(8,128)(2,1)S(1)}, u32[]{:S(2)}, u32[]{:S(2)}) %all-to-all-start) | async-done | bytes 524320 | tf_op jit(solution)/shard_map/all_to_all | solution.py:13
  153.6 1.2 gather_fusion.2
  154.8 1.2 gather_fusion.3
  155.9 0.1 copy.70
  156.1 1.5 broadcast_in_dim.115
  157.6 6.9 %all-to-all-start.1 = ((bf16[8,512,256]{1,2,0:T(8,128)(2,1)}), bf16[8,512,256]{1,2,0:T(8,128)(2,1)}, u32[]{:S(2)}, u32[]{:S(2)}) async-start(bf16[8,512,256]{1,2,0:T(8,128)(2,1)} %broadcast_in_dim.115), calls=%async_computation.1 | async-start | bytes 4194304 | tf_op jit(solution)/shard_map/all_to_all | solution.py:25
  164.5 12.7 %scatter_fusion.1 = s32[32,16]{0,1:T(8,128)S(1)} fusion(s32[32,16]{0,1:T(8,128)S(1)} %max.6, s32[256]{0:T(256)S(1)} %bitcast.89, s32[256]{0:T(256)S(1)} %iota.11), kind=kCustom, calls=%fused_computation.8 | custom fusion | bytes 5120 | tf_op jit(solution)/shard_map/scatter | solution.py:117
  177.4 38.8 %all-to-all-done.1 = bf16[8,512,256]{1,2,0:T(8,128)(2,1)} async-done(((bf16[8,512,256]{1,2,0:T(8,128)(2,1)}), bf16[8,512,256]{1,2,0:T(8,128)(2,1)}, u32[]{:S(2)}, u32[]{:S(2)}) %all-to-all-start.1) | async-done | bytes 2097184 | tf_op jit(solution)/shard_map/all_to_all | solution.py:25
  216.2 1.7 fusion.39
  217.9 0.7 fusion.1
  218.6 0.8 copy-done.8
  219.5 0.8 multiply_reduce_fusion
  220.3 0.6 broadcast_in_dim.121
  220.9 3.5 all-to-all-start.4
  224.5 13.1 %scatter_fusion = pred[32,16]{0,1:T(8,128)(4,1)S(1)} fusion(pred[32,16]{0,1:T(8,128)(4,1)S(1)} %broadcast_in_dim.109, s32[256]{0:T(256)S(1)} %bitcast.90, pred[256]{0:T(512)(128)(4,1)S(1)} %broadcast.271), kind=kCustom, calls=%fused_computation.7 | custom fusion | bytes 2816 | tf_op jit(solution)/shard_map/scatter | solution.py:119
  237.6 3.4 gather_fusion.6
  241.2 0.7 copy.76
  241.9 4.3 %all-to-all-start.5 = ((bf16[1,32,16]{2,0,1:T(2,128)(2,1)}), bf16[1,32,16]{2,0,1:T(2,128)(2,1)S(1)}, u32[]{:S(2)}, u32[]{:S(2)}) async-start(bf16[1,32,16]{2,0,1:T(2,128)(2,1)} %copy.76), calls=%async_computation.5 | async-start | bytes 32768 | tf_op jit(solution)/shard_map/all_to_all | solution.py:126
  246.2 0.8 convolution_convert_fusion
  247.0 1.1 copy.84
  248.1 9.8 %all-to-all-done.5 = bf16[1,32,16]{2,0,1:T(2,128)(2,1)S(1)} async-done(((bf16[1,32,16]{2,0,1:T(2,128)(2,1)}), bf16[1,32,16]{2,0,1:T(2,128)(2,1)S(1)}, u32[]{:S(2)}, u32[]{:S(2)}) %all-to-all-start.5) | async-done | bytes 1056 | tf_op jit(solution)/shard_map/all_to_all | solution.py:126
  257.9 6.7 %all-to-all-start.2 = ((bf16[8,256,256]{1,2,0:T(8,128)(2,1)}), bf16[8,256,256]{1,2,0:T(8,128)(2,1)S(1)}, u32[]{:S(2)}, u32[]{:S(2)}) async-start(bf16[8,256,256]{1,2,0:T(8,128)(2,1)} %bitcast.93), calls=%async_computation.2 | async-start | bytes 2097152 | tf_op jit(solution)/shard_map/all_to_all | solution.py:49
  264.9 25.9 %scatter_fusion.2 = f32[256,32]{0,1:T(8,128)S(1)} fusion(f32[256,32]{0,1:T(8,128)S(1)} %broadcast_in_dim.120, s32[512]{0:T(512)S(1)} %bitcast.91, f32[512]{0:T(512)S(1)} %broadcast_select_fusion.2), kind=kCustom, calls=%fused_computation.10 | custom fusion | flops 512 | bytes 10240 | tf_op jit(solution)/shard_map/scatter-add | solution.py:136
  291.0 2.8 all-to-all-done.2
  293.8 0.9 broadcast_in_dim.123
  294.7 4.9 %all-to-all-start.6 = ((bf16[32,256,32]{1,2,0:T(8,128)(2,1)}), bf16[32,256,32]{1,2,0:T(8,128)(2,1)}, u32[]{:S(2)}, u32[]{:S(2)}) async-start(bf16[32,256,32]{1,2,0:T(8,128)(2,1)} %broadcast_in_dim.123), calls=%async_computation.6 | async-start | bytes 1048576 | tf_op jit(solution)/shard_map/all_to_all | solution.py:25
  299.8 0.1 reduce_sum.49
  299.9 2.0 gather_fusion.4
  301.9 0.9 select_select_fusion
  302.8 30.3 %all-to-all-done.6 = bf16[32,256,32]{1,2,0:T(8,128)(2,1)} async-done(((bf16[32,256,32]{1,2,0:T(8,128)(2,1)}), bf16[32,256,32]{1,2,0:T(8,128)(2,1)}, u32[]{:S(2)}, u32[]{:S(2)}) %all-to-all-start.6) | async-done | bytes 524320 | tf_op jit(solution)/shard_map/all_to_all | solution.py:25
  333.1 4.5 %all-to-all-start.3 = ((bf16[256,32,16]{0,2,1:T(8,128)(2,1)}), bf16[256,32,16]{0,2,1:T(8,128)(2,1)S(1)}, u32[]{:S(2)}, u32[]{:S(2)}) async-start(bf16[256,32,16]{0,2,1:T(8,128)(2,1)} %select_select_fusion), calls=%async_computation.3 | async-start | bytes 524288 | tf_op jit(solution)/shard_map/all_to_all | solution.py:125
  337.6 4.5 %gather_fusion.5 = f32[512]{0:T(512)S(1)} fusion(f32[256,32]{0,1:T(8,128)S(1)} %get-tuple-element.10, s32[512]{0:T(512)S(1)} %bitcast.92), kind=kCustom, calls=%fused_computation.5 | custom fusion | bytes 8192 | tf_op jit(solution)/shard_map/gather | solution.py:132
  342.2 1.7 convert_reduce_fusion
  343.9 15.1 %all-to-all-done.3 = bf16[256,32,16]{0,2,1:T(8,128)(2,1)S(1)} async-done(((bf16[256,32,16]{0,2,1:T(8,128)(2,1)}), bf16[256,32,16]{0,2,1:T(8,128)(2,1)S(1)}, u32[]{:S(2)}, u32[]{:S(2)}) %all-to-all-start.3) | async-done | bytes 262176 | tf_op jit(solution)/shard_map/all_to_all | solution.py:125
  359.1 4.2 %scatter_custom_fusion.2 = f32[256,256]{0,1:T(8,128)S(1)} fusion(s32[512]{0:T(512)S(1)} %bitcast.106, bf16[256,512]{0,1:T(8,128)(2,1)S(1)} %bitcast.96, f32[512]{0:T(512)S(1)} %broadcast_select_fusion.3, f32[]{:T(128)} %constant.25.clone.1), kind=kCustom, calls=%fused_computation.41 | custom fusion | flops 393216 | bytes 526340 | tf_op jit(solution)/shard_map/scatter-add | solution.py:134
  363.3 0.9 convolution_add_fusion
  (67 shorter events, 2.0 us)
Async XLA Ops:
  0.6 217.3 %copy-start = (bf16[1,2048,512]{2,1,0:T(8,128)(2,1)S(1)}, bf16[1,2048,512]{2,1,0:T(8,128)(2,1)}, u32[]{:S(2)}) copy-start(bf16[1,2048,512]{2,1,0:T(8,128)(2,1)} %param.11) | copy-start | bytes 6291460
  35.1 3.6 copy-start.3
  35.1 3.7 %copy-start.7 = (s32[2]{0:T(128)S(1)}, s32[2]{0:T(128)}, u32[]{:S(2)}) copy-start(s32[2]{0:T(128)} %constant.90) | copy-start | bytes 28
  35.1 3.8 %copy-start.6 = (s32[2]{0:T(128)S(1)}, s32[2]{0:T(128)}, u32[]{:S(2)}) copy-start(s32[2]{0:T(128)} %constant.93) | copy-start | bytes 28
  35.1 34.7 %copy-start.2 = (bf16[256,256]{1,0:T(8,128)(2,1)S(1)}, bf16[256,256]{1,0:T(8,128)(2,1)}, u32[]{:S(2)}) copy-start(bf16[256,256]{1,0:T(8,128)(2,1)} %param.8) | copy-start | bytes 393220
  38.2 33.6 %copy-start.1 = (bf16[256,256]{1,0:T(8,128)(2,1)S(1)}, bf16[256,256]{1,0:T(8,128)(2,1)}, u32[]{:S(2)}) copy-start(bf16[256,256]{1,0:T(8,128)(2,1)} %param.7) | copy-start | bytes 393220
  74.9 78.6 %all-to-all-start = ((bf16[32,16,512]{2,1,0:T(8,128)(2,1)}), bf16[32,16,512]{2,1,0:T(8,128)(2,1)S(1)}, u32[]{:S(2)}, u32[]{:S(2)}) async-start(bf16[32,16,512]{2,1,0:T(8,128)(2,1)} %pad_maximum_fusion), calls=%async_computation | async-start | bytes 1048576 | tf_op jit(solution)/shard_map/all_to_all | solution.py:13
  157.6 58.7 %all-to-all-start.1 = ((bf16[8,512,256]{1,2,0:T(8,128)(2,1)}), bf16[8,512,256]{1,2,0:T(8,128)(2,1)}, u32[]{:S(2)}, u32[]{:S(2)}) async-start(bf16[8,512,256]{1,2,0:T(8,128)(2,1)} %broadcast_in_dim.115), calls=%async_computation.1 | async-start | bytes 4194304 | tf_op jit(solution)/shard_map/all_to_all | solution.py:25
  217.9 1.6 copy-start.8
  220.9 16.7 %all-to-all-start.4 = ((f32[8,1,256]{2,1,0:T(1,128)}), f32[8,1,256]{2,1,0:T(1,128)S(1)}, u32[]{:S(2)}, u32[]{:S(2)}) async-start(f32[8,1,256]{2,1,0:T(1,128)} %broadcast_in_dim.121), calls=%async_computation.4 | async-start | bytes 16384 | tf_op jit(solution)/shard_map/all_to_all | solution.py:25
  241.9 16.0 %all-to-all-start.5 = ((bf16[1,32,16]{2,0,1:T(2,128)(2,1)}), bf16[1,32,16]{2,0,1:T(2,128)(2,1)S(1)}, u32[]{:S(2)}, u32[]{:S(2)}) async-start(bf16[1,32,16]{2,0,1:T(2,128)(2,1)} %copy.76), calls=%async_computation.5 | async-start | bytes 32768 | tf_op jit(solution)/shard_map/all_to_all | solution.py:126
  257.9 35.9 %all-to-all-start.2 = ((bf16[8,256,256]{1,2,0:T(8,128)(2,1)}), bf16[8,256,256]{1,2,0:T(8,128)(2,1)S(1)}, u32[]{:S(2)}, u32[]{:S(2)}) async-start(bf16[8,256,256]{1,2,0:T(8,128)(2,1)} %bitcast.93), calls=%async_computation.2 | async-start | bytes 2097152 | tf_op jit(solution)/shard_map/all_to_all | solution.py:49
  264.9 25.9 %copy-start.4 = (f32[256,32]{0,1:T(8,128)S(1)}, f32[256,32]{0,1:T(8,128)}, u32[]{:S(2)}) copy-start(f32[256,32]{0,1:T(8,128)} %param.9) | copy-start | bytes 98308
  294.7 38.4 %all-to-all-start.6 = ((bf16[32,256,32]{1,2,0:T(8,128)(2,1)}), bf16[32,256,32]{1,2,0:T(8,128)(2,1)}, u32[]{:S(2)}, u32[]{:S(2)}) async-start(bf16[32,256,32]{1,2,0:T(8,128)(2,1)} %broadcast_in_dim.123), calls=%async_computation.6 | async-start | bytes 1048576 | tf_op jit(solution)/shard_map/all_to_all | solution.py:25
  302.8 60.5 %copy-start.5 = (bf16[256,32]{0,1:T(8,128)(2,1)S(1)}, bf16[256,32]{0,1:T(8,128)(2,1)}, u32[]{:S(2)}) copy-start(bf16[256,32]{0,1:T(8,128)(2,1)} %param.13) | copy-start | bytes 49156
  333.1 26.0 %all-to-all-start.3 = ((bf16[256,32,16]{0,2,1:T(8,128)(2,1)}), bf16[256,32,16]{0,2,1:T(8,128)(2,1)S(1)}, u32[]{:S(2)}, u32[]{:S(2)}) async-start(bf16[256,32,16]{0,2,1:T(8,128)(2,1)} %select_select_fusion), calls=%async_computation.3 | async-start | bytes 524288 | tf_op jit(solution)/shard_map/all_to_all | solution.py:125
where the time goes:
time: 367 us; the launch traced here: 364 us
  waiting for transfers between devices  130 us (35%)
  local copies, waits for them, and re-layouts  84.1 us (23%)
  starting transfers between devices  76.1 us (21%)
  other arithmetic  69.2 us (19%)
    all_to_all x3, waiting for transfers between devices, copy_for_each(): return lax.all_to_all(copies, axis, split_axis=0, concat_axis=0, tiled=True)  69.1 us
    all_to_all x1, starting transfers between devices, in_one_piece(): lax.all_to_all(both, axis, split_axis=split_dim, concat_axis=concat_dim,...  45.2 us
    all_to_all x1, waiting for transfers between devices, in_one_piece(): lax.all_to_all(both, axis, split_axis=split_dim, concat_axis=concat_dim,...  33.4 us
    another operation x2, other arithmetic  32.4 us
    unnamed x21, local copies, waits for them, and re-layouts  31.4 us
    scatter-add x1, other arithmetic, per_device(): jnp.zeros((tok_dev, experts), jnp.float32).at[flat_tok, expert_of]  25.9 us
    all_to_all x3, starting transfers between devices, copy_for_each(): return lax.all_to_all(copies, axis, split_axis=0, concat_axis=0, tiled=True)  15.3 us
    all_to_all x1, waiting for transfers between devices, per_device(): lax.all_to_all(send_contrib, 'expert', split_axis=1, concat_axis=1, tiled...  15.1 us
  transfers between devices with their start and end apart: 7, of which 6 were waited for; matrix products, arithmetic and copies ran while one was open for 17% of the time, Pallas kernels for 0%

commit v1 on v0

v1 whole, which is shorter than its diff:
```python
import jax
import jax.numpy as jnp
from jax import lax
from jax.sharding import PartitionSpec as P

inv_root_two = 0.7071067811865476
inv_root_tau = 0.3989422804014327
LANES = 128
EXTRA = 8
f32 = jnp.float32
bf16 = jnp.bfloat16


def mm(a, b, contract=((1,), (0,))):
    return lax.dot_general(a, b, (contract, ((), ())), preferred_element_type=f32)


def gelu_parts(hidden_pre):
    cumulative = 0.5 * (1.0 + lax.erf(hidden_pre * inv_root_two))
    slopes = cumulative + hidden_pre * jnp.exp(-0.5 * hidden_pre * hidden_pre) * inv_root_tau
    return (hidden_pre * cumulative, slopes)


def in_parts(v, parts):
    out = []
    for _ in range(parts):
        part = lax.reduce_precision(v, 8, 7)
        out.append(part.astype(bf16))
        v = v - part
    return out


def lane_blocks(x):
    return [x[:, k : k + LANES] for k in range(0, x.shape[1], LANES)]


def pack_source(tokens, grads, logits, indices, here):
    tok, _ = tokens.shape
    experts, capacity = indices.shape
    most = min(tok, 2 * capacity // experts)
    local = indices - here * tok
    token_range = jnp.arange(tok, dtype=jnp.int32)
    member = jnp.any(local[:, :, None] == token_range[None, None, :], axis=1)
    before = (token_range[:, None] < token_range[None, :]).astype(bf16)
    rank = mm(member.astype(bf16), before).astype(jnp.int32)
    rank = jnp.where(member, rank, -1)
    ranks = jnp.arange(most, dtype=jnp.int32)
    hits = rank[:, None, :] == ranks[None, :, None]
    pick = hits.astype(bf16).reshape(experts * most, tok)
    blocks = [
        mm(pick, b).astype(bf16).reshape(experts, most, LANES)
        for b in lane_blocks(tokens) + lane_blocks(grads)
    ]
    probs = jax.nn.sigmoid(logits).T
    slot_probs = jnp.sum(jnp.where(hits, probs[:, None, :], 0.0), axis=2)
    extra = jnp.stack(in_parts(slot_probs, 3), axis=1)
    blocks.append(jnp.pad(extra, ((0, 0), (0, EXTRA - 3), (0, LANES - most))))
    return jnp.concatenate(blocks, axis=1), pick


def compact(recv, own, tok, most):
    sources = recv.shape[0]
    capacity = own.shape[0]
    src = own // tok
    s_range = jnp.arange(sources, dtype=jnp.int32)
    count = jnp.sum((src[:, None] == s_range[None, :]).astype(jnp.int32), axis=0)
    end = jnp.sum(jnp.where(s_range[:, None] <= s_range[None, :], count[:, None], 0), axis=0)
    start = end - count
    slot = jnp.arange(capacity, dtype=jnp.int32)
    of_source = (slot[:, None] >= start[None, :]) & (slot[:, None] < end[None, :])
    within = slot - jnp.sum(jnp.where(of_source, start[None, :], 0), axis=1)
    lanes = jnp.arange(LANES, dtype=jnp.int32)
    n_rows = recv.shape[1] - EXTRA
    ext = recv[:, n_rows : n_rows + 3, :]
    table = mm(of_source.astype(bf16), ext.reshape(sources, 3 * LANES))
    table = sum(lane_blocks(table))
    probs = jnp.sum(jnp.where(lanes[None, :] == within[:, None], table, 0.0), axis=1)
    ranks = jnp.arange(most, dtype=jnp.int32)
    place = jnp.where(ranks[None, :] < count[:, None], start[:, None] + ranks[None, :], -1)
    place = (slot[:, None, None] == place[None, :, :]).astype(bf16)
    place = place.reshape(capacity, sources * most)
    rows = [
        mm(place, recv[:, k : k + most, :].reshape(sources * most, LANES)).astype(bf16)
        for k in range(0, n_rows, most)
    ]
    return jnp.concatenate(rows, axis=1), probs, place


def gathered(x, axis):
    return lax.all_gather(x, axis)


def hidden_part(rows, weight_in, weight_out):
    devices, capacity, both = rows.shape
    cols = both // 2
    xs = jnp.moveaxis(rows[:, :, :cols], 0, 1).reshape(capacity, devices * cols)
    dys = jnp.moveaxis(rows[:, :, cols:], 0, 1).reshape(capacity, devices * cols)
    pre = mm(xs, weight_in)
    back = mm(dys, weight_out, ((1,), (1,)))
    activated, slopes = gelu_parts(pre)
    gates = jnp.sum(activated * back, axis=1)
    delta = (back * slopes).astype(bf16)
    contrib = mm(delta, weight_in, ((1,), (1,))).astype(bf16)
    contrib = contrib.reshape(capacity, devices, cols // LANES, LANES)
    contrib = contrib.transpose(1, 2, 0, 3).reshape(devices, cols // LANES * capacity, LANES)
    extra = jnp.concatenate([p.reshape(capacity // LANES, LANES) for p in in_parts(gates, 3)])
    extra = jnp.pad(extra, ((0, EXTRA - extra.shape[0]), (0, 0)))
    extra = jnp.broadcast_to(extra[None], (devices, *extra.shape))
    return jnp.concatenate([contrib, extra], axis=1)


def combine(parts, probs, own_x, router_col, place, most):
    capacity, cols = own_x.shape
    total = jnp.sum(parts.astype(f32), axis=0)
    blocks = cols // LANES
    extra = total[blocks * capacity :]
    per = capacity // LANES
    gates = (extra[:per] + extra[per : 2 * per] + extra[2 * per : 3 * per]).reshape(capacity)
    logit_grad = (probs * (1.0 - probs) * gates).astype(bf16)
    column = mm(logit_grad[None, :], own_x)
    sources = place.shape[1] // most
    out = []
    for k in range(blocks):
        block = total[k * capacity : (k + 1) * capacity] * probs[:, None]
        block = block + logit_grad.astype(f32)[:, None] * router_col[None, k * LANES : (k + 1) * LANES]
        block = mm(place, block.astype(bf16), ((0,), (0,))).astype(bf16)
        out.append(block.reshape(sources, most, LANES))
    extra = jnp.concatenate([p.reshape(blocks, LANES) for p in in_parts(column[0], 2)])
    extra = jnp.pad(extra, ((0, EXTRA - extra.shape[0]), (0, 0)))
    out.append(jnp.broadcast_to(extra[None], (sources, *extra.shape)))
    return jnp.concatenate(out, axis=1)


def finish(recv, pick, cols, most):
    experts = recv.shape[0]
    blocks = cols // LANES
    rows = [
        recv[:, k * most : (k + 1) * most, :].reshape(experts * most, LANES) for k in range(blocks)
    ]
    input_grad = mm(pick, jnp.concatenate(rows, axis=1), ((0,), (0,)))
    extra = recv[:, blocks * most :, :].astype(f32)
    column = extra[:, :blocks, :] + extra[:, blocks : 2 * blocks, :]
    return input_grad, column.reshape(experts, cols).T


def per_device(tokens_in, out_grad, logits, indices, w_in, w_out, router_w):
    tok, cols = tokens_in.shape
    experts, capacity = indices.shape
    most = min(tok, 2 * capacity // experts)
    here = lax.axis_index("expert")
    own = lax.dynamic_index_in_dim(indices, here, 0, keepdims=False)
    send, pick = pack_source(tokens_in, out_grad, logits, indices, here)
    recv = lax.all_to_all(send, "expert", 0, 0, tiled=True)
    rows, probs, place = compact(recv, own, tok, most)
    parts = hidden_part(gathered(rows, "mp"), w_in[0], w_out[0])
    parts = lax.all_to_all(parts, "mp", 0, 0, tiled=True)
    e_range = jnp.arange(experts, dtype=jnp.int32)
    router_col = jnp.sum(jnp.where(e_range[None, :] == here, router_w.astype(f32), 0.0), axis=1)
    back = combine(parts, probs, rows[:, :cols], router_col, place, most)
    back = lax.all_to_all(back, "expert", 0, 0, tiled=True)
    return finish(back, pick, cols, most)


def solution(mesh):
    return jax.shard_map(
        per_device,
        mesh=mesh,
        in_specs=(
            P(("groups", "expert"), "mp"),
            P(("groups", "expert"), "mp"),
            P(("groups", "expert"), None),
            P("groups", None),
            P("expert", None, "mp"),
            P("expert", "mp", None),
            P("mp", None),
        ),
        out_specs=(P(("groups", "expert"), "mp"), P(("groups", "mp"), None)),
        check_vma=False,
    )
```

time: 367 us -> 236 us (0.64)
  local copies, waits for them, and re-layouts: 84.1 us -> 11.8 us
  other arithmetic: 69.2 us -> 6.05 us
  blocking collectives: 0 us -> 42.4 us
  waiting for transfers between devices: 130 us -> 100 us
  starting transfers between devices: 76.1 us -> 49.1 us
  between operations: 1.13 us -> 14.4 us
  matrix products: 3.41 us -> 11.5 us
    all_to_all x7 -> x2, waiting for transfers between devices: 130 us -> 58.7 us  [the longest x1 35.2 us: per_device(): recv = lax.all_to_all(send, 'expert', 0, 0, tiled=True)]
    all_to_all x0 -> x1, blocking collectives: none -> 42.4 us  [per_device(): back = lax.all_to_all(back, 'expert', 0, 0, tiled=True)]
    all_gather x0 -> x1, waiting for transfers between devices: none -> 41.4 us  [gathered(): return lax.all_gather(x, axis)]
    another operation x2 -> x1, other arithmetic: 32.4 us -> 0.01 us  [pack_source(): extra = jnp.stack(in_parts(slot_probs, 3), axis=1)]
    scatter-add x2 -> x0, other arithmetic: 30.1 us -> none  [the longest x1 25.9 us: per_device(): jnp.zeros((tok_dev, experts), jnp.float32).at[flat_tok, expert_of]]
    all_to_all x7 -> x2, starting transfers between devices: 76.1 us -> 49.1 us  [the longest x1 45.2 us: per_device(): recv = lax.all_to_all(send, 'expert', 0, 0, tiled=True)]
    scatter x4 -> x0, local copies, waits for them, and re-layouts: 26 us -> none  [the longest x2 13.2 us: per_device(): jnp.zeros((experts, most_rows), jnp.bool_).at[own_src, own_rank].set(True)]
    unnamed x21 -> x17, local copies, waits for them, and re-layouts: 31.4 us -> 6.95 us
  transfers between devices with their start and end apart: 7 -> 3, of which waited for: 6 -> 3; matrix products, arithmetic and copies ran while one was open for 17% -> 1% of each run, Pallas kernels for 0% -> 0%
where the time goes in v1:
time: 236 us
  waiting for transfers between devices  100 us (42%)
  starting transfers between devices  49.1 us (21%)
  blocking collectives  42.4 us (18%)
  between operations  14.4 us (6%)
  local copies, waits for them, and re-layouts  11.8 us (5%)
  matrix products  11.5 us (5%)
  other arithmetic  6.05 us (3%)
    all_to_all x1, starting transfers between devices, per_device(): recv = lax.all_to_all(send, 'expert', 0, 0, tiled=True)  45.2 us
    all_to_all x1, blocking collectives, per_device(): back = lax.all_to_all(back, 'expert', 0, 0, tiled=True)  42.4 us
    all_gather x1, waiting for transfers between devices, gathered(): return lax.all_gather(x, axis)  41.4 us
    all_to_all x1, waiting for transfers between devices, per_device(): recv = lax.all_to_all(send, 'expert', 0, 0, tiled=True)  35.2 us
    all_to_all x1, waiting for transfers between devices, per_device(): parts = lax.all_to_all(parts, 'mp', 0, 0, tiled=True)  23.6 us
    dot_general x17, matrix products, mm(): lax.dot_general(a, b, (contract, ((), ())), preferred_element_type=f32)  11.5 us
    unnamed x17, local copies, waits for them, and re-layouts  6.95 us
  transfers between devices with their start and end apart: 3, of which 3 were waited for; matrix products, arithmetic and copies ran while one was open for 1% of the time, Pallas kernels for 0%

profile of v1, /device:TPU:65, one launch (start us, length us, event | category | flops | bytes accessed | tf_op | source)
XLA Modules:
  0.0 235.6 jit_solution(16208213892286443610)
XLA Ops:
  7.3 0.9 broadcast_subtract_fusion
  8.2 1.4 fusion
  9.6 0.2 fusion.10
  9.8 0.1 bitcast_compare_fusion
  9.9 1.1 convolution_convert_fusion.3
  11.0 1.1 convolution_convert_fusion.4
  12.1 1.1 convolution_convert_fusion.5
  13.2 1.1 convolution_convert_fusion.6
  14.2 0.8 divide_bitcast_fusion
  15.0 0.1 select_reduce_fusion
  15.2 0.7 constant_dynamic-update-slice_fusion.3
  15.9 0.7 constant_dynamic-update-slice_fusion.2
  16.6 0.7 constant_dynamic-update-slice_fusion.1
  17.3 0.7 constant_dynamic-update-slice_fusion
  18.0 0.7 pad_dynamic-update-slice_fusion
  18.7 45.2 %all-to-all-start = ((bf16[32,72,128]{2,1,0:T(8,128)(2,1)}), bf16[32,72,128]{2,1,0:T(8,128)(2,1)S(1)}, u32[]{:S(2)}, u32[]{:S(2)}) async-start(bf16[32,72,128]{2,1,0:T(8,128)(2,1)} %pad_dynamic-update-slice_fusion), calls=%async_computation | async-start | bytes 1179648 | tf_op jit(solution)/shard_map/all_to_all | solution.py:153
  63.9 0.7 constant_dynamic-slice_fusion
  64.7 0.1 convert_reduce_fusion.1
  64.9 35.2 %all-to-all-done = bf16[32,72,128]{2,1,0:T(8,128)(2,1)S(1)} async-done(((bf16[32,72,128]{2,1,0:T(8,128)(2,1)}), bf16[32,72,128]{2,1,0:T(8,128)(2,1)S(1)}, u32[]{:S(2)}, u32[]{:S(2)}) %all-to-all-start) | async-done | bytes 589856 | tf_op jit(solution)/shard_map/all_to_all | solution.py:153
  100.1 0.3 fusion.6
  100.4 0.3 fusion.7
  100.7 0.3 fusion.8
  101.0 0.3 fusion.9
  101.4 0.7 pad_maximum_fusion.2
  102.1 41.4 %all-gather.3.cloned.1.call-done = bf16[2048,512]{0,1:T(8,128)(2,1)} async-done(((bf16[256,512]{0,1:T(8,128)(2,1)}), bf16[2048,512]{0,1:T(8,128)(2,1)}) %all-gather.3.cloned.1.call-update) | async-done | bytes 2097168 | tf_op jit(solution)/shard_map/all_gather | solution.py:90
  143.6 2.3 copy.62
  145.9 0.1 fusion.88
  146.0 0.2 copy.60
  146.2 0.2 copy.59
  146.5 0.7 fusion.2
  147.2 0.8 copy-done.3
  148.0 0.9 multiply_reduce_fusion
  148.9 1.8 convolution_convert_fusion
  150.7 1.8 reshape.232
  152.5 0.3 copy.54
  152.8 1.1 pad_maximum_fusion
  153.9 3.9 %all-to-all-start.1 = ((bf16[8,520,128]{2,1,0:T(8,128)(2,1)}), bf16[8,520,128]{2,1,0:T(8,128)(2,1)S(1)}, u32[]{:S(2)}, u32[]{:S(2)}) async-start(bf16[8,520,128]{2,1,0:T(8,128)(2,1)} %pad_maximum_fusion), calls=%async_computation.1 | async-start | bytes 2129920 | tf_op jit(solution)/shard_map/all_to_all | solution.py:156
  158.3 0.9 slice.117
  159.1 0.3 fusion.57
  159.5 0.2 fusion.33
  159.7 23.6 %all-to-all-done.1 = bf16[8,520,128]{2,1,0:T(8,128)(2,1)S(1)} async-done(((bf16[8,520,128]{2,1,0:T(8,128)(2,1)}), bf16[8,520,128]{2,1,0:T(8,128)(2,1)S(1)}, u32[]{:S(2)}, u32[]{:S(2)}) %all-to-all-start.1) | async-done | bytes 1064992 | tf_op jit(solution)/shard_map/all_to_all | solution.py:156
  183.2 0.1 convert_reduce_fusion
  183.4 0.1 fusion.36
  183.6 0.5 convolution_convert_fusion.1
  184.0 0.4 convolution_convert_fusion.2
  184.6 42.4 %all_to_all.15 = bf16[32,40,128]{2,1,0:T(8,128)(2,1)S(1)} all-to-all(bf16[32,40,128]{2,1,0:T(8,128)(2,1)S(1)} %pad_maximum_fusion.1), channel_id=1, replica_groups=mesh['groups'=2,'expert'=32,'mp'=8] {'expert'}, dimensions={0} | all-to-all | bytes 655360 | tf_op jit(solution)/shard_map/all_to_all | solution.py:160
  227.0 0.6 copy.78
  227.7 1.0 fusion.18
  (41 shorter events, 1.1 us)
Async XLA Ops:
  7.2 139.3 %copy-start = (bf16[1,2048,512]{2,1,0:T(8,128)(2,1)S(1)}, bf16[1,2048,512]{2,1,0:T(8,128)(2,1)}, u32[]{:S(2)}) copy-start(bf16[1,2048,512]{2,1,0:T(8,128)(2,1)} %param.11) | copy-start | bytes 6291460
  18.7 81.4 %all-to-all-start = ((bf16[32,72,128]{2,1,0:T(8,128)(2,1)}), bf16[32,72,128]{2,1,0:T(8,128)(2,1)S(1)}, u32[]{:S(2)}, u32[]{:S(2)}) async-start(bf16[32,72,128]{2,1,0:T(8,128)(2,1)} %pad_dynamic-update-slice_fusion), calls=%async_computation | async-start | bytes 1179648 | tf_op jit(solution)/shard_map/all_to_all | solution.py:153
  63.9 79.7 %all-gather.3.cloned.1.call-start = ((), (), s32[]{:S(2)}) async-start(), calls=%async_computation.3 | async-start | bytes 2359296 | tf_op jit(solution)/shard_map/all_gather | solution.py:90
  100.1 45.8 %copy-start.1 = (bf16[32,72,128]{2,1,0:T(8,128)(2,1)}, bf16[32,72,128]{2,1,0:T(8,128)(2,1)S(1)}, u32[]{:S(2)}) copy-start(bf16[32,72,128]{2,1,0:T(8,128)(2,1)S(1)} %all-to-all-done) | copy-start | bytes 1769476
  146.4 1.6 copy-start.3
  152.8 5.3 %copy-start.2 = (bf16[256,32]{0,1:T(8,128)(2,1)S(1)}, bf16[256,32]{0,1:T(8,128)(2,1)}, u32[]{:S(2)}) copy-start(bf16[256,32]{0,1:T(8,128)(2,1)} %param.13) | copy-start | bytes 49156
  153.9 29.4 %all-to-all-start.1 = ((bf16[8,520,128]{2,1,0:T(8,128)(2,1)}), bf16[8,520,128]{2,1,0:T(8,128)(2,1)S(1)}, u32[]{:S(2)}, u32[]{:S(2)}) async-start(bf16[8,520,128]{2,1,0:T(8,128)(2,1)} %pad_maximum_fusion), calls=%async_computation.1 | async-start | bytes 2129920 | tf_op jit(solution)/shard_map/all_to_all | solution.py:156
Sparse Core Ops, SparseCore 0:
  102.3 41.2 all-gather.2
